TPU v7x, 32 devices: a whole 2x2x4 slice. The times are simulated.
32 devices in a mesh: gx: 4 (over z), gy: 4 (over x, core), gz: 2 (over y).
Axes of the slice: x: 2, y: 2, z: 4, core: 2. Of those that a mesh axis runs over, the one named last changes fastest.
Arguments:
- models: float32 [2, 64, 128, 256], P(None, 'gx', 'gy', 'gz'), may hold values from -6 to 6
- targets: float32 [2, 64, 128, 256], P(None, 'gx', 'gy', 'gz'), may hold values from -6 to 6
- weights: float32 [2, 64, 128, 256], P(None, 'gx', 'gy', 'gz'), may hold values from 0.5 to 12, as said below
Outputs:
- updated: float32 [2, 64, 128, 256], P(None, 'gx', 'gy', 'gz')
- applied_last: float32 [2, 64, 128, 256], P(None, 'gx', 'gy', 'gz')
Inputs may be any that keep to these rules, and one draw needn't show every extreme that they name: Positive data weights.
All inputs are finite; a program needn't handle non-finite values.
Results may differ from a plain program's by a relative error of at most 0.00016.
Values sent between devices are 32-bit elements; how exact they have to be, the bound alone decides.
A program may use at most 128 MiB of HBM per device.

v0:
```python
import functools

import jax
import jax.numpy as jnp
from jax import lax
from jax.experimental import pallas as pl
from jax.experimental.pallas import tpu as pltpu
from jax.sharding import PartitionSpec as P

ITERS = 3
AXES = ("gx", "gy", "gz")
MESH = pl.DeviceIdType.MESH
X1, X2, Y, Z, YE, ZE = 0, 2, 4, 6, 8, 10
COUPLE = -2.0 * 0.05 / 16.0


def kernel(sizes, models, targets, weights, updated, applied, cur, grad, zcur, zgrad, pack, f0, f1, f2, fz,
           ysend, yrecv, yesend, yerecv, zsend, zrecv, red, send, recv, red_send, red_recv):
    nx, ny, nz = sizes
    total = nx * ny * nz
    _, cells_x, cells_y, lanes = models.shape
    low, high = 8, 8 + cells_y
    own = pl.ds(low, cells_y)
    ix, iy, iz = (lax.axis_index(axis) for axis in AXES)
    here = (ix, iy, iz)
    me = (ix * ny + iy) * nz + iz
    lane_row = lax.broadcasted_iota(jnp.int32, (1, lanes), 1)
    slot = lax.rem(lane_row, 4)

    def has(axis, direction):
        return here[axis] > 0 if direction == 0 else here[axis] < sizes[axis] - 1

    def copy(step, axis, direction, kind, src, dst):
        there = list(here)
        there[axis] = here[axis] + (1 if direction else -1)
        return pltpu.make_async_remote_copy(
            src_ref=src, dst_ref=dst, send_sem=send.at[step, kind + direction], recv_sem=recv.at[step, kind + direction],
            device_id=tuple(there), device_id_type=MESH)

    def transfers(step, field):
        made = {}
        for direction in range(2):
            near, far = (2, cells_x + 2) if direction == 0 else (cells_x + 1, 1)
            made[X1, direction] = (0, field.at[:, near, own], field.at[:, far, own])
            near, far = (3, cells_x + 3) if direction == 0 else (cells_x, 0)
            made[X2, direction] = (0, field.at[:, near, own], field.at[:, far, own])
            made[Y, direction] = (1, ysend.at[step, direction], yrecv.at[step, direction])
            made[YE, direction] = (1, yesend.at[step, direction], yerecv.at[step, direction])
            made[Z, direction] = (2, zsend.at[step, 0], zrecv.at[step, 0, direction])
            made[ZE, direction] = (2, zsend.at[step, 1], zrecv.at[step, 1, direction])
        return {key: (value[0], copy(step, value[0], key[1], key[0], value[1], value[2])) for key, value in made.items()}

    def start(made, kind):
        for direction in range(2):
            axis, move = made[kind, direction]

            @pl.when(has(axis, direction))
            def _():
                move.start()

    def arrive(made, kind):
        for direction in range(2):
            axis, move = made[kind, direction]

            @pl.when(has(axis, 1 - direction))
            def _():
                move.wait_recv()

    def sent(made, kind):
        for direction in range(2):
            axis, move = made[kind, direction]

            @pl.when(has(axis, direction))
            def _():
                move.wait_send()

    def pack_z(field, step, which):
        group = lane_row // 4

        def body(xi, carry):
            return tuple(
                jnp.where(group == xi, pltpu.roll(field[m, xi], 4 * xi + 2, 1), carry[m]) for m in range(2))

        zero = jnp.zeros(field.shape[2:], jnp.float32)
        edge = 2 if which == 0 else 1
        packed = lax.fori_loop(edge, cells_x + 4 - edge, body, (zero, zero))
        for m in range(2):
            v = packed[m]
            pack[m] = v
            turned = jnp.where(slot == 0, pltpu.roll(v, lanes - 3, 1), pltpu.roll(v, 3, 1))
            turned = jnp.where(slot == 1, pltpu.roll(v, lanes - 1, 1), turned)
            zsend[step, which, m] = jnp.where(slot == 2, pltpu.roll(v, 1, 1), turned)

    def unpack_z(zfield, step, which):
        for m in range(2):
            zfield[m] = jnp.where(slot >= 2, zrecv[step, which, 1, m], zrecv[step, which, 0, m])

    def phase_a(made, field, zfield, step):
        start(made, X1)
        for m in range(2):
            for x in range(cells_x):
                ysend[step, 0, m, 2 * x:2 * x + 2] = field[m, x + 2, low:low + 2]
                ysend[step, 1, m, 2 * x:2 * x + 2] = field[m, x + 2, high - 2:high]
        start(made, Y)
        pack_z(field, step, 0)
        start(made, Z)
        start(made, X2)
        arrive(made, Y)
        for m in range(2):
            for x in range(cells_x):
                field[m, x + 2, low - 2:low] = yrecv[step, 1, m, 2 * x:2 * x + 2]
                field[m, x + 2, high:high + 2] = yrecv[step, 0, m, 2 * x:2 * x + 2]
        arrive(made, Z)
        unpack_z(zfield, step, 0)
        arrive(made, X1)

    def phase_b_start(made, field, step):
        for m in range(2):
            for side, xi in enumerate((1, cells_x + 2)):
                at = 2 * m + side
                yesend[step, 0, at:at + 1] = field[m, xi, low:low + 1]
                yesend[step, 1, at:at + 1] = field[m, xi, high - 1:high]
        start(made, YE)
        pack_z(field, step, 1)
        start(made, ZE)

    def phase_b_end(made, field, zfield, step):
        arrive(made, YE)
        for m in range(2):
            for side, xi in enumerate((1, cells_x + 2)):
                at = 2 * m + side
                field[m, xi, low - 1:low] = yerecv[step, 1, at:at + 1]
                field[m, xi, high:high + 1] = yerecv[step, 0, at:at + 1]
        arrive(made, ZE)
        unpack_z(zfield, step, 1)
        arrive(made, X2)

    def turn(packed, xi):
        return pltpu.roll(packed, lanes - 2 - 4 * xi, 1)

    def up(v, halo):
        return jnp.where(lane_row == lanes - 1, halo, pltpu.roll(v, lanes - 1, 1))

    def down(v, halo):
        return jnp.where(lane_row == 0, halo, pltpu.roll(v, 1, 1))

    def cross(a, b, k):
        i, j = (k + 1) % 3, (k + 2) % 3
        return a[i] * b[j] - a[j] * b[i]

    def flux_pass():
        def z_halo():
            diffs = []
            rows, above, below = own, pl.ds(low + 1, cells_y), pl.ds(low - 1, cells_y)
            for m in range(2):
                halo, edge = zcur[m, rows], pack[m, rows]
                diffs.append((
                    pltpu.roll(halo, lanes - 4, 1) - pltpu.roll(halo, 4, 1),
                    zcur[m, above] - zcur[m, below],
                    jnp.where(slot == 1, pltpu.roll(halo, 1, 1) - edge, edge - pltpu.roll(halo, lanes - 1, 1))))
            a, b = diffs
            crossed = [cross(a, b, k) for k in range(3)]
            fz[0, :] = cross(b, crossed, 2)
            fz[1, :] = cross(crossed, a, 2)

        z_halo()

        def rows_flux(xi, first, count, comps):
            rows = pl.ds(first, count)
            diffs = []
            for m in range(2):
                v = cur[m, xi, rows]
                halo = turn(zcur[m, rows], xi)
                diffs.append((
                    cur[m, xi + 1, rows] - cur[m, xi - 1, rows],
                    cur[m, xi, pl.ds(first + 1, count)] - cur[m, xi, pl.ds(first - 1, count)],
                    up(v, halo) - down(v, halo)))
            a, b = diffs
            crossed = [cross(a, b, k) for k in range(3)]
            for k in comps:
                one, two = cross(b, crossed, k), cross(crossed, a, k)
                if k == 0:
                    f0[0, xi], f0[1, xi] = one, two
                elif k == 1:
                    f1[0, xi, rows], f1[1, xi, rows] = one, two
                else:
                    f2[0, xi], f2[1, xi] = one, two

        def body(xi, carry):
            rows_flux(xi, low, cells_y, (0, 1, 2))
            rows_flux(xi, low - 1, 1, (1,))
            rows_flux(xi, high, 1, (1,))
            return carry

        rows_flux(1, low, cells_y, (0,))
        lax.fori_loop(2, cells_x + 2, body, 0)
        rows_flux(cells_x + 2, low, cells_y, (0,))

    def fold(v):
        return jnp.sum(v.reshape(cells_y // 8, 8, lanes), axis=0)

    def laplace(field, zfield, m, xi):
        v = field[m, xi, own]
        halo = turn(zfield[m, own], xi)
        around = field[m, xi + 1, own] + field[m, xi - 1, own]
        around = around + (field[m, xi, pl.ds(low + 1, cells_y)] + field[m, xi, pl.ds(low - 1, cells_y)])
        return v, 6.0 * v - (around + (up(v, halo) + down(v, halo)))

    def gradient_pass(step):
        def body(xi, norm):
            for m in range(2):
                v, smooth = laplace(cur, zcur, m, xi)
                inner = f2[m, xi]
                halo = turn(fz[m], xi)
                div = f0[m, xi + 1] - f0[m, xi - 1]
                div = div + (f1[m, xi, pl.ds(low + 1, cells_y)] - f1[m, xi, pl.ds(low - 1, cells_y)])
                div = div + (up(inner, halo) - down(inner, halo))
                g = weights[m, xi - 2] * (v - targets[m, xi - 2]) + smooth + COUPLE * div
                grad[step, m, xi, own] = g
                norm = norm + fold(g * g)
            return norm

        return lax.fori_loop(2, cells_x + 2, body, jnp.zeros((8, lanes), jnp.float32))

    def curvature_pass(step):
        def body(xi, curve):
            for m in range(2):
                v, smooth = laplace(grad.at[step], zgrad, m, xi)
                turned = weights[m, xi - 2] * v + smooth
                if step == ITERS - 1:
                    applied[m, xi - 2] = turned
                curve = curve + fold(v * turned)
            return curve

        return lax.fori_loop(2, cells_x + 2, body, jnp.zeros((8, lanes), jnp.float32))

    def red_copy(step, k):
        peer = lax.rem(me + k, total)
        there = (peer // (ny * nz), lax.rem(peer // nz, ny), lax.rem(peer, nz))
        return pltpu.make_async_remote_copy(
            src_ref=red.at[step, me], dst_ref=red.at[step, me], send_sem=red_send.at[step], recv_sem=red_recv.at[step],
            device_id=there, device_id_type=MESH)

    def reduce_start(step, norm, curve):
        row = jnp.where(lane_row < lanes // 2, jnp.sum(norm), jnp.sum(curve))
        red[step, me] = row

        def body(k, carry):
            red_copy(step, k).start()
            return carry

        lax.fori_loop(1, total, body, 0)

    def reduce_wait(step, sem):
        part = red.at[step, pl.ds(0, total - 1)]
        pltpu.make_async_copy(part, part, sem.at[step]).wait()

    def reduce_end(step):
        reduce_wait(step, red_recv)
        summed = jnp.sum(red[step], axis=0)
        ratio = summed / pltpu.roll(summed, lanes // 2, 1)
        return jnp.where(lane_row < lanes // 2, ratio, pltpu.roll(ratio, lanes // 2, 1))

    first, last = transfers(0, cur), []
    zgrad[...] = jnp.zeros_like(zgrad)
    for m in range(2):
        def load(xi, carry):
            cur[m, xi, own] = models[m, xi - 2]
            return carry
        lax.fori_loop(2, cells_x + 2, load, 0)
    phase_a(first, cur, zcur, 0)
    phase_b_start(first, cur, 0)
    phase_b_end(first, cur, zcur, 0)
    last.append((first, True))

    for step in range(ITERS):
        final = step == ITERS - 1
        flux_pass()
        norm = gradient_pass(step)
        field = grad.at[step]
        made = transfers(step + 1, field)
        phase_a(made, field, zgrad, step + 1)
        curve = curvature_pass(step)
        reduce_start(step, norm, curve)
        last.append((made, not final))
        if not final:
            phase_b_start(made, field, step + 1)
            phase_b_end(made, field, zgrad, step + 1)
            alpha = reduce_end(step)
            if step == 0:
                sent(first, X1)
                sent(first, X2)

            def move(xi, carry):
                for m in range(2):
                    cur[m, xi] = cur[m, xi] - alpha * grad[step, m, xi]
                return carry

            lax.fori_loop(0, cells_x + 4, move, 0)
            for m in range(2):
                zcur[m] = zcur[m] - alpha * zgrad[m]
            pack_z(cur, 0, 2)
        else:
            arrive(made, X2)
            alpha = reduce_end(step)

            def finish(x, carry):
                for m in range(2):
                    updated[m, x] = cur[m, x + 2, own] - alpha * grad[step, m, x + 2, own]
                return carry

            lax.fori_loop(0, cells_x, finish, 0)

    for made, both in last:
        faces = (Y, Z) if made is first else (X1, X2, Y, Z)
        for kind in faces + ((YE, ZE) if both else ()):
            sent(made, kind)
    for step in range(ITERS):
        reduce_wait(step, red_send)


def clearing(sizes, *refs):
    models, targets, weights, updated, applied, cur, grad = refs[:7]
    yrecv, yesend, yerecv, zrecv = refs[14], refs[15], refs[16], refs[18]
    for ref in (yrecv, yesend, yerecv, zrecv):
        ref[...] = jnp.zeros(ref.shape, jnp.float32)
    cells_x = models.shape[1]

    def body(xi, carry):
        for m in range(2):
            cur[m, xi] = jnp.zeros(cur.shape[2:], jnp.float32)
            for step in range(ITERS):
                grad[step, m, xi] = jnp.zeros(cur.shape[2:], jnp.float32)
        return carry

    lax.fori_loop(0, cells_x + 4, body, 0)
    total = sizes[0] * sizes[1] * sizes[2]
    ix, iy, iz = (lax.axis_index(axis) for axis in AXES)
    me = (ix * sizes[1] + iy) * sizes[2] + iz
    barrier = pltpu.get_barrier_semaphore()

    def greet(k, carry):
        peer = lax.rem(me + k, total)
        there = (peer // (sizes[1] * sizes[2]), lax.rem(peer // sizes[2], sizes[1]), lax.rem(peer, sizes[2]))
        pl.semaphore_signal(barrier, inc=1, device_id=there, device_id_type=MESH)
        return carry

    lax.fori_loop(1, total, greet, 0)
    pl.semaphore_wait(barrier, total - 1)
    kernel(sizes, *refs)


def solution(mesh):
    sizes = tuple(mesh.shape[axis] for axis in AXES)

    def local(models, targets, weights):
        _, nx, ny, nz = models.shape
        rows = ny + 16
        total = sizes[0] * sizes[1] * sizes[2]
        steps = ITERS + 1
        whole = pl.BlockSpec(memory_space=pltpu.VMEM)
        f32 = jnp.float32
        return pl.pallas_call(
            functools.partial(clearing, sizes),
            out_shape=(jax.ShapeDtypeStruct(models.shape, f32),) * 2,
            in_specs=[whole] * 3,
            out_specs=(whole, whole),
            scratch_shapes=[
                pltpu.VMEM((2, nx + 4, rows, nz), f32),
                pltpu.VMEM((ITERS, 2, nx + 4, rows, nz), f32),
                pltpu.VMEM((2, rows, nz), f32),
                pltpu.VMEM((2, rows, nz), f32),
                pltpu.VMEM((2, rows, nz), f32),
                pltpu.VMEM((2, nx + 4, ny, nz), f32),
                pltpu.VMEM((2, nx + 4, rows, nz), f32),
                pltpu.VMEM((2, nx + 4, ny, nz), f32),
                pltpu.VMEM((2, ny, nz), f32),
                pltpu.VMEM((steps, 2, 2, 2 * nx, nz), f32),
                pltpu.VMEM((steps, 2, 2, 2 * nx, nz), f32),
                pltpu.VMEM((steps, 2, 8, nz), f32),
                pltpu.VMEM((steps, 2, 8, nz), f32),
                pltpu.VMEM((steps, 3, 2, rows, nz), f32),
                pltpu.VMEM((steps, 2, 2, 2, rows, nz), f32),
                pltpu.VMEM((ITERS, total, 1, nz), f32),
                pltpu.SemaphoreType.DMA((steps, 12)),
                pltpu.SemaphoreType.DMA((steps, 12)),
                pltpu.SemaphoreType.DMA((ITERS,)),
                pltpu.SemaphoreType.DMA((ITERS,)),
            ],
            compiler_params=pltpu.CompilerParams(
                collective_id=0, has_side_effects=True, vmem_limit_bytes=48 * 1024 * 1024),
        )(models, targets, weights)

    spec = P(None, *AXES)
    return jax.shard_map(local, mesh=mesh, in_specs=(spec,) * 3, out_specs=(spec, spec), check_vma=False)
```

profile of v0, /device:TPU:0, one launch (start us, length us, event | category | flops | bytes accessed | tf_op | source)
XLA Modules:
  0.0 73.6 jit_solution(8309817535302957839)
XLA Ops:
  0.6 0.0 copy-start
  0.6 1.0 %copy-done = f32[2,16,32,128]{3,2,1,0:T(8,128)S(1)} copy-done((f32[2,16,32,128]{3,2,1,0:T(8,128)S(1)}, f32[2,16,32,128]{3,2,1,0:T(8,128)}, u32[]{:S(2)}) %copy-start) | copy-done | bytes 524312
  1.7 0.0 copy-start.1
  1.7 1.0 %copy-done.1 = f32[2,16,32,128]{3,2,1,0:T(8,128)S(1)} copy-done((f32[2,16,32,128]{3,2,1,0:T(8,128)S(1)}, f32[2,16,32,128]{3,2,1,0:T(8,128)}, u32[]{:S(2)}) %copy-start.1) | copy-done | bytes 524312
  2.7 0.0 copy-start.2
  2.7 1.0 %copy-done.2 = f32[2,16,32,128]{3,2,1,0:T(8,128)S(1)} copy-done((f32[2,16,32,128]{3,2,1,0:T(8,128)S(1)}, f32[2,16,32,128]{3,2,1,0:T(8,128)}, u32[]{:S(2)}) %copy-start.2) | copy-done | bytes 524312
  3.8 68.2 %shard_map.50 = (f32[2,16,32,128]{3,2,1,0:T(8,128)S(1)}, f32[2,16,32,128]{3,2,1,0:T(8,128)S(1)}) custom-call(f32[2,16,32,128]{3,2,1,0:T(8,128)S(1)} %copy-done, f32[2,16,32,128]{3,2,1,0:T(8,128)S(1)} %copy-done.1, f32[2,16,32,128]{3,2,1,0:T(8,128)S(1)} %copy-done.2), custom_call_target="tpu_custom_call" | custom-call | tf_op jit(solution)/shard_map/pallas_call | solution.py:363
  72.0 0.8 %copy.7 = f32[2,16,32,128]{3,2,1,0:T(8,128)} copy(f32[2,16,32,128]{3,2,1,0:T(8,128)S(1)} %get-tuple-element.4) | data formatting | bytes 1048576
  72.8 0.8 %copy.8 = f32[2,16,32,128]{3,2,1,0:T(8,128)} copy(f32[2,16,32,128]{3,2,1,0:T(8,128)S(1)} %get-tuple-element.5) | data formatting | bytes 1048576
Async XLA Ops:
  0.6 1.0 %copy-start = (f32[2,16,32,128]{3,2,1,0:T(8,128)S(1)}, f32[2,16,32,128]{3,2,1,0:T(8,128)}, u32[]{:S(2)}) copy-start(f32[2,16,32,128]{3,2,1,0:T(8,128)} %refs_0_.1) | copy-start | bytes 1572868
  1.7 1.0 %copy-start.1 = (f32[2,16,32,128]{3,2,1,0:T(8,128)S(1)}, f32[2,16,32,128]{3,2,1,0:T(8,128)}, u32[]{:S(2)}) copy-start(f32[2,16,32,128]{3,2,1,0:T(8,128)} %refs_1_.1) | copy-start | bytes 1572868
  2.7 1.0 %copy-start.2 = (f32[2,16,32,128]{3,2,1,0:T(8,128)S(1)}, f32[2,16,32,128]{3,2,1,0:T(8,128)}, u32[]{:S(2)}) copy-start(f32[2,16,32,128]{3,2,1,0:T(8,128)} %refs_2_.1) | copy-start | bytes 1572868
where the time goes:
time: 73.8 us; the launch traced here: 73.6 us
  Pallas kernels  68.2 us (92%)
  local copies, waits for them, and re-layouts  4.71 us (6%)
    pallas_call x1, Pallas kernels, local(): pl.pallas_call(functools.partial(clearing, sizes), out_shape=(jax.ShapeDt...  68.2 us
    unnamed x8, local copies, waits for them, and re-layouts  4.71 us

commit v1 on v0

--- a/solution.py
+++ b/solution.py
@@ -14,16 +14,15 @@
 COUPLE = -2.0 * 0.05 / 16.0
 
 
-def kernel(sizes, models, targets, weights, updated, applied, cur, grad, zcur, zgrad, pack, f0, f1, f2, fz,
-           ysend, yrecv, yesend, yerecv, zsend, zrecv, red, send, recv, red_send, red_recv):
+def kernel(sizes, models, targets_in, weights_in, updated, applied, cur, grad, zcur, zgrad, pack, f0, f1, f2, fz,
+           ysend, yrecv, yesend, yerecv, zsend, zrecv, targets, weights, red, line, send, recv, red_send, red_recv,
+           line_send, line_recv, fetched):
     nx, ny, nz = sizes
-    total = nx * ny * nz
     _, cells_x, cells_y, lanes = models.shape
     low, high = 8, 8 + cells_y
     own = pl.ds(low, cells_y)
     ix, iy, iz = (lax.axis_index(axis) for axis in AXES)
     here = (ix, iy, iz)
-    me = (ix * ny + iy) * nz + iz
     lane_row = lax.broadcasted_iota(jnp.int32, (1, lanes), 1)
     slot = lax.rem(lane_row, 4)
 
@@ -106,13 +105,29 @@
         start(made, Z)
         start(made, X2)
         arrive(made, Y)
+        arrive(made, Z)
+        unpack_z(zfield, step, 0)
+        arrive(made, X1)
+
+    def unpack_y(field, step):
         for m in range(2):
             for x in range(cells_x):
                 field[m, x + 2, low - 2:low] = yrecv[step, 1, m, 2 * x:2 * x + 2]
                 field[m, x + 2, high:high + 2] = yrecv[step, 0, m, 2 * x:2 * x + 2]
-        arrive(made, Z)
-        unpack_z(zfield, step, 0)
-        arrive(made, X1)
+
+    def face_terms(field, step):
+        row = lax.broadcasted_iota(jnp.int32, (2 * cells_x, 1), 0)
+        even = lax.rem(row, 2) == 0
+        inner = jnp.logical_or(slot == 1, slot == 2)
+        count = 2 * cells_x
+        terms = jnp.zeros((8, lanes), jnp.float32)
+        for m in range(2):
+            terms = terms + fold(field[m, 2, own] * field[m, 1, own] + field[m, cells_x + 1, own] * field[m, cells_x + 2, own])
+            before = ysend[step, 0, m] * pltpu.roll(yrecv[step, 1, m], count - 1, 0)
+            after = ysend[step, 1, m] * pltpu.roll(yrecv[step, 0, m], 1, 0)
+            terms = terms + jnp.sum(jnp.where(even, before, after).reshape(count // 8, 8, lanes), axis=0)
+            terms = terms + fold(jnp.where(inner, pack[m, own] * zgrad[m, own], 0.0))
+        return terms
 
     def phase_b_start(made, field, step):
         for m in range(2):
@@ -121,8 +136,6 @@
                 yesend[step, 0, at:at + 1] = field[m, xi, low:low + 1]
                 yesend[step, 1, at:at + 1] = field[m, xi, high - 1:high]
         start(made, YE)
-        pack_z(field, step, 1)
-        start(made, ZE)
 
     def phase_b_end(made, field, zfield, step):
         arrive(made, YE)
@@ -207,7 +220,9 @@
         return v, 6.0 * v - (around + (up(v, halo) + down(v, halo)))
 
     def gradient_pass(step):
-        def body(xi, norm):
+        def body(xi, carry):
+            norm, curve, edges, before = carry
+            kept = []
             for m in range(2):
                 v, smooth = laplace(cur, zcur, m, xi)
                 inner = f2[m, xi]
@@ -215,76 +230,130 @@
                 div = f0[m, xi + 1] - f0[m, xi - 1]
                 div = div + (f1[m, xi, pl.ds(low + 1, cells_y)] - f1[m, xi, pl.ds(low - 1, cells_y)])
                 div = div + (up(inner, halo) - down(inner, halo))
-                g = weights[m, xi - 2] * (v - targets[m, xi - 2]) + smooth + COUPLE * div
+                weight = weights[m, xi - 2]
+                g = weight * (v - targets[m, xi - 2]) + smooth + COUPLE * div
                 grad[step, m, xi, own] = g
-                norm = norm + fold(g * g)
-            return norm
-
-        return lax.fori_loop(2, cells_x + 2, body, jnp.zeros((8, lanes), jnp.float32))
-
-    def curvature_pass(step):
-        def body(xi, curve):
+                square = g * g
+                norm = norm + fold(square)
+                curve = curve + fold((weight + 6.0) * square)
+                later = jnp.where(row_in == cells_y - 1, 0.0, pltpu.roll(g, cells_y - 1, 0))
+                beside = jnp.where(lane_row == lanes - 1, 0.0, pltpu.roll(g, lanes - 1, 1))
+                edges = edges + fold(g * (before[m] + later + beside))
+                kept.append(g)
+            return norm, curve, edges, tuple(kept)
+
+        row_in = lax.broadcasted_iota(jnp.int32, (cells_y, 1), 0)
+        zero, slab = jnp.zeros((8, lanes), jnp.float32), jnp.zeros((cells_y, lanes), jnp.float32)
+        norm, curve, edges, _ = lax.fori_loop(2, cells_x + 2, body, (zero, zero, zero, (slab, slab)))
+        return norm, curve - 2.0 * edges
+
+    def applied_pass(step):
+        def body(xi, carry):
             for m in range(2):
                 v, smooth = laplace(grad.at[step], zgrad, m, xi)
-                turned = weights[m, xi - 2] * v + smooth
-                if step == ITERS - 1:
-                    applied[m, xi - 2] = turned
-                curve = curve + fold(v * turned)
-            return curve
-
-        return lax.fori_loop(2, cells_x + 2, body, jnp.zeros((8, lanes), jnp.float32))
-
-    def red_copy(step, k):
-        peer = lax.rem(me + k, total)
-        there = (peer // (ny * nz), lax.rem(peer // nz, ny), lax.rem(peer, nz))
+                applied[m, xi - 2] = weights[m, xi - 2] * v + smooth
+            return carry
+
+        lax.fori_loop(2, cells_x + 2, body, 0)
+
+    plane, place = ny * nz, iy * nz + iz
+
+    def plane_copy(step, k):
+        peer = lax.rem(place + k, plane)
         return pltpu.make_async_remote_copy(
-            src_ref=red.at[step, me], dst_ref=red.at[step, me], send_sem=red_send.at[step], recv_sem=red_recv.at[step],
-            device_id=there, device_id_type=MESH)
-
-    def reduce_start(step, norm, curve):
-        row = jnp.where(lane_row < lanes // 2, jnp.sum(norm), jnp.sum(curve))
-        red[step, me] = row
-
-        def body(k, carry):
-            red_copy(step, k).start()
-            return carry
-
-        lax.fori_loop(1, total, body, 0)
-
-    def reduce_wait(step, sem):
-        part = red.at[step, pl.ds(0, total - 1)]
-        pltpu.make_async_copy(part, part, sem.at[step]).wait()
+            src_ref=red.at[step, place], dst_ref=red.at[step, place], send_sem=red_send.at[step],
+            recv_sem=red_recv.at[step], device_id=(ix, peer // nz, lax.rem(peer, nz)), device_id_type=MESH)
+
+    def line_copy(step, k):
+        return pltpu.make_async_remote_copy(
+            src_ref=line.at[step, ix], dst_ref=line.at[step, ix], send_sem=line_send.at[step],
+            recv_sem=line_recv.at[step], device_id=(lax.rem(ix + k, nx), iy, iz), device_id_type=MESH)
+
+    def reduce_wait(ref, step, count, sem):
+        if count > 1:
+            part = ref.at[step, pl.ds(0, count - 1)]
+            pltpu.make_async_copy(part, part, sem.at[step]).wait()
+
+    def reduce_plane(step, norm, curve):
+        red[step, place] = jnp.where(lane_row < lanes // 2, jnp.sum(norm), jnp.sum(curve))
+        for k in range(1, plane):
+            plane_copy(step, k).start()
+
+    def reduce_line(step):
+        reduce_wait(red, step, plane, red_recv)
+        line[step, ix] = jnp.sum(red[step], axis=0)
+        for k in range(1, nx):
+            line_copy(step, k).start()
 
     def reduce_end(step):
-        reduce_wait(step, red_recv)
-        summed = jnp.sum(red[step], axis=0)
+        reduce_wait(line, step, nx, line_recv)
+        summed = jnp.sum(line[step], axis=0)
         ratio = summed / pltpu.roll(summed, lanes // 2, 1)
         return jnp.where(lane_row < lanes // 2, ratio, pltpu.roll(ratio, lanes // 2, 1))
 
+    fetches = [
+        pltpu.make_async_copy(models, cur.at[:, pl.ds(2, cells_x), own], fetched.at[0]),
+        pltpu.make_async_copy(weights_in, weights, fetched.at[1]),
+        pltpu.make_async_copy(targets_in, targets, fetched.at[2]),
+    ]
+    for fetch in fetches:
+        fetch.start()
+    for ref in (yrecv, yesend, yerecv, zrecv):
+        ref[...] = jnp.zeros(ref.shape, jnp.float32)
+    blank = jnp.zeros(cur.shape[2:], jnp.float32)
+    for m in range(2):
+        for xi in (0, 1, cells_x + 2, cells_x + 3):
+            cur[m, xi] = blank
+            for step in range(ITERS):
+                grad[step, m, xi] = blank
+    barrier = pltpu.get_barrier_semaphore()
+    for k in range(1, plane):
+        peer = lax.rem(place + k, plane)
+        pl.semaphore_signal(
+            barrier, inc=1, device_id=(ix, peer // nz, lax.rem(peer, nz)), device_id_type=MESH)
+    for k in range(1, nx):
+        pl.semaphore_signal(barrier, inc=1, device_id=(lax.rem(ix + k, nx), iy, iz), device_id_type=MESH)
+    strip = jnp.zeros((8, lanes), jnp.float32)
+
+    def clear(xi, carry):
+        for m in range(2):
+            for at in (0, high):
+                cur[m, xi, at:at + 8] = strip
+                for step in range(ITERS):
+                    grad[step, m, xi, at:at + 8] = strip
+        return carry
+
+    lax.fori_loop(2, cells_x + 2, clear, 0)
+    zgrad[...] = jnp.zeros_like(zgrad)
+    fetches[0].wait()
+    pl.semaphore_wait(barrier, plane + nx - 2)
+
     first, last = transfers(0, cur), []
-    zgrad[...] = jnp.zeros_like(zgrad)
-    for m in range(2):
-        def load(xi, carry):
-            cur[m, xi, own] = models[m, xi - 2]
-            return carry
-        lax.fori_loop(2, cells_x + 2, load, 0)
     phase_a(first, cur, zcur, 0)
     phase_b_start(first, cur, 0)
+    unpack_y(cur, 0)
+    pack_z(cur, 0, 1)
+    start(first, ZE)
     phase_b_end(first, cur, zcur, 0)
     last.append((first, True))
+    fetches[1].wait()
+    fetches[2].wait()
 
     for step in range(ITERS):
         final = step == ITERS - 1
         flux_pass()
-        norm = gradient_pass(step)
+        norm, curve = gradient_pass(step)
         field = grad.at[step]
         made = transfers(step + 1, field)
         phase_a(made, field, zgrad, step + 1)
-        curve = curvature_pass(step)
-        reduce_start(step, norm, curve)
+        reduce_plane(step, norm, curve - face_terms(field, step + 1))
         last.append((made, not final))
         if not final:
             phase_b_start(made, field, step + 1)
+            unpack_y(field, step + 1)
+            reduce_line(step)
+            pack_z(field, step + 1, 1)
+            start(made, ZE)
             phase_b_end(made, field, zgrad, step + 1)
             alpha = reduce_end(step)
             if step == 0:
@@ -301,6 +370,9 @@
                 zcur[m] = zcur[m] - alpha * zgrad[m]
             pack_z(cur, 0, 2)
         else:
+            unpack_y(field, step + 1)
+            reduce_line(step)
+            applied_pass(step)
             arrive(made, X2)
             alpha = reduce_end(step)
 
@@ -316,38 +388,8 @@
         for kind in faces + ((YE, ZE) if both else ()):
             sent(made, kind)
     for step in range(ITERS):
-        reduce_wait(step, red_send)
-
-
-def clearing(sizes, *refs):
-    models, targets, weights, updated, applied, cur, grad = refs[:7]
-    yrecv, yesend, yerecv, zrecv = refs[14], refs[15], refs[16], refs[18]
-    for ref in (yrecv, yesend, yerecv, zrecv):
-        ref[...] = jnp.zeros(ref.shape, jnp.float32)
-    cells_x = models.shape[1]
-
-    def body(xi, carry):
-        for m in range(2):
-            cur[m, xi] = jnp.zeros(cur.shape[2:], jnp.float32)
-            for step in range(ITERS):
-                grad[step, m, xi] = jnp.zeros(cur.shape[2:], jnp.float32)
-        return carry
-
-    lax.fori_loop(0, cells_x + 4, body, 0)
-    total = sizes[0] * sizes[1] * sizes[2]
-    ix, iy, iz = (lax.axis_index(axis) for axis in AXES)
-    me = (ix * sizes[1] + iy) * sizes[2] + iz
-    barrier = pltpu.get_barrier_semaphore()
-
-    def greet(k, carry):
-        peer = lax.rem(me + k, total)
-        there = (peer // (sizes[1] * sizes[2]), lax.rem(peer // sizes[2], sizes[1]), lax.rem(peer, sizes[2]))
-        pl.semaphore_signal(barrier, inc=1, device_id=there, device_id_type=MESH)
-        return carry
-
-    lax.fori_loop(1, total, greet, 0)
-    pl.semaphore_wait(barrier, total - 1)
-    kernel(sizes, *refs)
+        reduce_wait(red, step, plane, red_send)
+        reduce_wait(line, step, nx, line_send)
 
 
 def solution(mesh):
@@ -356,14 +398,13 @@
     def local(models, targets, weights):
         _, nx, ny, nz = models.shape
         rows = ny + 16
-        total = sizes[0] * sizes[1] * sizes[2]
         steps = ITERS + 1
         whole = pl.BlockSpec(memory_space=pltpu.VMEM)
         f32 = jnp.float32
         return pl.pallas_call(
-            functools.partial(clearing, sizes),
+            functools.partial(kernel, sizes),
             out_shape=(jax.ShapeDtypeStruct(models.shape, f32),) * 2,
-            in_specs=[whole] * 3,
+            in_specs=[pl.BlockSpec(memory_space=pl.ANY)] * 3,
             out_specs=(whole, whole),
             scratch_shapes=[
                 pltpu.VMEM((2, nx + 4, rows, nz), f32),
@@ -381,11 +422,17 @@
                 pltpu.VMEM((steps, 2, 8, nz), f32),
                 pltpu.VMEM((steps, 3, 2, rows, nz), f32),
                 pltpu.VMEM((steps, 2, 2, 2, rows, nz), f32),
-                pltpu.VMEM((ITERS, total, 1, nz), f32),
+                pltpu.VMEM((2, nx, ny, nz), f32),
+                pltpu.VMEM((2, nx, ny, nz), f32),
+                pltpu.VMEM((ITERS, sizes[1] * sizes[2], 1, nz), f32),
+                pltpu.VMEM((ITERS, sizes[0], 1, nz), f32),
                 pltpu.SemaphoreType.DMA((steps, 12)),
                 pltpu.SemaphoreType.DMA((steps, 12)),
                 pltpu.SemaphoreType.DMA((ITERS,)),
                 pltpu.SemaphoreType.DMA((ITERS,)),
+                pltpu.SemaphoreType.DMA((ITERS,)),
+                pltpu.SemaphoreType.DMA((ITERS,)),
+                pltpu.SemaphoreType.DMA((3,)),
             ],
             compiler_params=pltpu.CompilerParams(
                 collective_id=0, has_side_effects=True, vmem_limit_bytes=48 * 1024 * 1024),

time: 73.8 us -> 76.9 us (1.042)
  Pallas kernels: 68.2 us -> 71.3 us
    pallas_call x1, Pallas kernels: 68.2 us -> 71.3 us  [local(): pl.pallas_call(functools.partial(kernel, sizes), out_shape=(jax.ShapeDtyp...]
where the time goes in v1:
time: 76.9 us; the launch traced here: 76.6 us
  Pallas kernels  71.3 us (93%)
  local copies, waits for them, and re-layouts  4.71 us (6%)
    pallas_call x1, Pallas kernels, local(): pl.pallas_call(functools.partial(kernel, sizes), out_shape=(jax.ShapeDtyp...  71.3 us
    unnamed x8, local copies, waits for them, and re-layouts  4.71 us

profile of v1, /device:TPU:0, one launch (start us, length us, event | category | flops | bytes accessed | tf_op | source)
XLA Modules:
  0.0 76.6 jit_solution(1214221366055334871)
XLA Ops:
  0.6 0.0 copy-start
  0.6 1.0 %copy-done = f32[2,16,32,128]{3,2,1,0:T(8,128)S(1)} copy-done((f32[2,16,32,128]{3,2,1,0:T(8,128)S(1)}, f32[2,16,32,128]{3,2,1,0:T(8,128)}, u32[]{:S(2)}) %copy-start) | copy-done | bytes 524312
  1.7 0.0 copy-start.1
  1.7 1.0 %copy-done.1 = f32[2,16,32,128]{3,2,1,0:T(8,128)S(1)} copy-done((f32[2,16,32,128]{3,2,1,0:T(8,128)S(1)}, f32[2,16,32,128]{3,2,1,0:T(8,128)}, u32[]{:S(2)}) %copy-start.1) | copy-done | bytes 524312
  2.7 0.0 copy-start.2
  2.7 1.0 %copy-done.2 = f32[2,16,32,128]{3,2,1,0:T(8,128)S(1)} copy-done((f32[2,16,32,128]{3,2,1,0:T(8,128)S(1)}, f32[2,16,32,128]{3,2,1,0:T(8,128)}, u32[]{:S(2)}) %copy-start.2) | copy-done | bytes 524312
  3.8 71.3 %shard_map.50 = (f32[2,16,32,128]{3,2,1,0:T(8,128)S(1)}, f32[2,16,32,128]{3,2,1,0:T(8,128)S(1)}) custom-call(f32[2,16,32,128]{3,2,1,0:T(8,128)S(1)} %copy-done, f32[2,16,32,128]{3,2,1,0:T(8,128)S(1)} %copy-done.1, f32[2,16,32,128]{3,2,1,0:T(8,128)S(1)} %copy-done.2), custom_call_target="tpu_custom_call" | custom-call | tf_op jit(solution)/shard_map/pallas_call | solution.py:404
  75.1 0.8 %copy.7 = f32[2,16,32,128]{3,2,1,0:T(8,128)} copy(f32[2,16,32,128]{3,2,1,0:T(8,128)S(1)} %get-tuple-element.4) | data formatting | bytes 1048576
  75.9 0.8 %copy.8 = f32[2,16,32,128]{3,2,1,0:T(8,128)} copy(f32[2,16,32,128]{3,2,1,0:T(8,128)S(1)} %get-tuple-element.5) | data formatting | bytes 1048576
Async XLA Ops:
  0.6 1.0 %copy-start = (f32[2,16,32,128]{3,2,1,0:T(8,128)S(1)}, f32[2,16,32,128]{3,2,1,0:T(8,128)}, u32[]{:S(2)}) copy-start(f32[2,16,32,128]{3,2,1,0:T(8,128)} %models.1) | copy-start | bytes 1572868
  1.7 1.0 %copy-start.1 = (f32[2,16,32,128]{3,2,1,0:T(8,128)S(1)}, f32[2,16,32,128]{3,2,1,0:T(8,128)}, u32[]{:S(2)}) copy-start(f32[2,16,32,128]{3,2,1,0:T(8,128)} %targets_in.1) | copy-start | bytes 1572868
  2.7 1.0 %copy-start.2 = (f32[2,16,32,128]{3,2,1,0:T(8,128)S(1)}, f32[2,16,32,128]{3,2,1,0:T(8,128)}, u32[]{:S(2)}) copy-start(f32[2,16,32,128]{3,2,1,0:T(8,128)} %weights_in.1) | copy-start | bytes 1572868

commit v2 on v1

--- a/solution.py
+++ b/solution.py
@@ -15,8 +15,8 @@
 
 
 def kernel(sizes, models, targets_in, weights_in, updated, applied, cur, grad, zcur, zgrad, pack, f0, f1, f2, fz,
-           ysend, yrecv, yesend, yerecv, zsend, zrecv, targets, weights, red, line, send, recv, red_send, red_recv,
-           line_send, line_recv, fetched):
+           ysend, yrecv, yesend, yerecv, zsend, zrecv, targets, weights, red, send, recv, red_send, red_recv,
+           fetched):
     nx, ny, nz = sizes
     _, cells_x, cells_y, lanes = models.shape
     low, high = 8, 8 + cells_y
@@ -82,7 +82,9 @@
 
         zero = jnp.zeros(field.shape[2:], jnp.float32)
         edge = 2 if which == 0 else 1
-        packed = lax.fori_loop(edge, cells_x + 4 - edge, body, (zero, zero))
+        packed = (zero, zero)
+        for xi in range(edge, cells_x + 4 - edge):
+            packed = body(xi, packed)
         for m in range(2):
             v = packed[m]
             pack[m] = v
@@ -206,7 +208,7 @@
             return carry
 
         rows_flux(1, low, cells_y, (0,))
-        lax.fori_loop(2, cells_x + 2, body, 0)
+        lax.fori_loop(2, cells_x + 2, body, 0, unroll=4)
         rows_flux(cells_x + 2, low, cells_y, (0,))
 
     def fold(v):
@@ -244,7 +246,7 @@
 
         row_in = lax.broadcasted_iota(jnp.int32, (cells_y, 1), 0)
         zero, slab = jnp.zeros((8, lanes), jnp.float32), jnp.zeros((cells_y, lanes), jnp.float32)
-        norm, curve, edges, _ = lax.fori_loop(2, cells_x + 2, body, (zero, zero, zero, (slab, slab)))
+        norm, curve, edges, _ = lax.fori_loop(2, cells_x + 2, body, (zero, zero, zero, (slab, slab)), unroll=4)
         return norm, curve - 2.0 * edges
 
     def applied_pass(step):
@@ -254,20 +256,15 @@
                 applied[m, xi - 2] = weights[m, xi - 2] * v + smooth
             return carry
 
-        lax.fori_loop(2, cells_x + 2, body, 0)
-
-    plane, place = ny * nz, iy * nz + iz
+        lax.fori_loop(2, cells_x + 2, body, 0, unroll=4)
+
+    plane, place = nx * ny * nz, (ix * ny + iy) * nz + iz
 
     def plane_copy(step, k):
         peer = lax.rem(place + k, plane)
         return pltpu.make_async_remote_copy(
             src_ref=red.at[step, place], dst_ref=red.at[step, place], send_sem=red_send.at[step],
-            recv_sem=red_recv.at[step], device_id=(ix, peer // nz, lax.rem(peer, nz)), device_id_type=MESH)
-
-    def line_copy(step, k):
-        return pltpu.make_async_remote_copy(
-            src_ref=line.at[step, ix], dst_ref=line.at[step, ix], send_sem=line_send.at[step],
-            recv_sem=line_recv.at[step], device_id=(lax.rem(ix + k, nx), iy, iz), device_id_type=MESH)
+            recv_sem=red_recv.at[step], device_id=(peer // (ny * nz), lax.rem(peer // nz, ny), lax.rem(peer, nz)), device_id_type=MESH)
 
     def reduce_wait(ref, step, count, sem):
         if count > 1:
@@ -279,15 +276,9 @@
         for k in range(1, plane):
             plane_copy(step, k).start()
 
-    def reduce_line(step):
+    def reduce_end(step):
         reduce_wait(red, step, plane, red_recv)
-        line[step, ix] = jnp.sum(red[step], axis=0)
-        for k in range(1, nx):
-            line_copy(step, k).start()
-
-    def reduce_end(step):
-        reduce_wait(line, step, nx, line_recv)
-        summed = jnp.sum(line[step], axis=0)
+        summed = jnp.sum(red[step], axis=0)
         ratio = summed / pltpu.roll(summed, lanes // 2, 1)
         return jnp.where(lane_row < lanes // 2, ratio, pltpu.roll(ratio, lanes // 2, 1))
 
@@ -310,9 +301,7 @@
     for k in range(1, plane):
         peer = lax.rem(place + k, plane)
         pl.semaphore_signal(
-            barrier, inc=1, device_id=(ix, peer // nz, lax.rem(peer, nz)), device_id_type=MESH)
-    for k in range(1, nx):
-        pl.semaphore_signal(barrier, inc=1, device_id=(lax.rem(ix + k, nx), iy, iz), device_id_type=MESH)
+            barrier, inc=1, device_id=(peer // (ny * nz), lax.rem(peer // nz, ny), lax.rem(peer, nz)), device_id_type=MESH)
     strip = jnp.zeros((8, lanes), jnp.float32)
 
     def clear(xi, carry):
@@ -326,7 +315,7 @@
     lax.fori_loop(2, cells_x + 2, clear, 0)
     zgrad[...] = jnp.zeros_like(zgrad)
     fetches[0].wait()
-    pl.semaphore_wait(barrier, plane + nx - 2)
+    pl.semaphore_wait(barrier, plane - 1)
 
     first, last = transfers(0, cur), []
     phase_a(first, cur, zcur, 0)
@@ -351,7 +340,6 @@
         if not final:
             phase_b_start(made, field, step + 1)
             unpack_y(field, step + 1)
-            reduce_line(step)
             pack_z(field, step + 1, 1)
             start(made, ZE)
             phase_b_end(made, field, zgrad, step + 1)
@@ -365,13 +353,12 @@
                     cur[m, xi] = cur[m, xi] - alpha * grad[step, m, xi]
                 return carry
 
-            lax.fori_loop(0, cells_x + 4, move, 0)
+            lax.fori_loop(0, cells_x + 4, move, 0, unroll=2)
             for m in range(2):
                 zcur[m] = zcur[m] - alpha * zgrad[m]
             pack_z(cur, 0, 2)
         else:
             unpack_y(field, step + 1)
-            reduce_line(step)
             applied_pass(step)
             arrive(made, X2)
             alpha = reduce_end(step)
@@ -381,7 +368,7 @@
                     updated[m, x] = cur[m, x + 2, own] - alpha * grad[step, m, x + 2, own]
                 return carry
 
-            lax.fori_loop(0, cells_x, finish, 0)
+            lax.fori_loop(0, cells_x, finish, 0, unroll=2)
 
     for made, both in last:
         faces = (Y, Z) if made is first else (X1, X2, Y, Z)
@@ -389,7 +376,6 @@
             sent(made, kind)
     for step in range(ITERS):
         reduce_wait(red, step, plane, red_send)
-        reduce_wait(line, step, nx, line_send)
 
 
 def solution(mesh):
@@ -424,12 +410,9 @@
                 pltpu.VMEM((steps, 2, 2, 2, rows, nz), f32),
                 pltpu.VMEM((2, nx, ny, nz), f32),
                 pltpu.VMEM((2, nx, ny, nz), f32),
-                pltpu.VMEM((ITERS, sizes[1] * sizes[2], 1, nz), f32),
-                pltpu.VMEM((ITERS, sizes[0], 1, nz), f32),
+                pltpu.VMEM((ITERS, sizes[0] * sizes[1] * sizes[2], 1, nz), f32),
                 pltpu.SemaphoreType.DMA((steps, 12)),
                 pltpu.SemaphoreType.DMA((steps, 12)),
-                pltpu.SemaphoreType.DMA((ITERS,)),
-                pltpu.SemaphoreType.DMA((ITERS,)),
                 pltpu.SemaphoreType.DMA((ITERS,)),
                 pltpu.SemaphoreType.DMA((ITERS,)),
                 pltpu.SemaphoreType.DMA((3,)),

time: 76.9 us -> 56.9 us (0.74)
  Pallas kernels: 71.3 us -> 51.2 us
    pallas_call x1, Pallas kernels: 71.3 us -> 51.2 us  [local(): pl.pallas_call(functools.partial(kernel, sizes), out_shape=(jax.ShapeDtyp...]
where the time goes in v2:
time: 56.9 us; the launch traced here: 56.6 us
  Pallas kernels  51.2 us (90%)
  local copies, waits for them, and re-layouts  4.71 us (8%)
  between operations  0.65 us (1%)
    pallas_call x1, Pallas kernels, local(): pl.pallas_call(functools.partial(kernel, sizes), out_shape=(jax.ShapeDtyp...  51.2 us
    unnamed x8, local copies, waits for them, and re-layouts  4.71 us

profile of v2, /device:TPU:0, one launch (start us, length us, event | category | flops | bytes accessed | tf_op | source)
XLA Modules:
  0.0 56.6 jit_solution(5141282333959090739)
XLA Ops:
  0.6 0.0 copy-start
  0.6 1.0 %copy-done = f32[2,16,32,128]{3,2,1,0:T(8,128)S(1)} copy-done((f32[2,16,32,128]{3,2,1,0:T(8,128)S(1)}, f32[2,16,32,128]{3,2,1,0:T(8,128)}, u32[]{:S(2)}) %copy-start) | copy-done | bytes 524312
  1.7 0.0 copy-start.1
  1.7 1.0 %copy-done.1 = f32[2,16,32,128]{3,2,1,0:T(8,128)S(1)} copy-done((f32[2,16,32,128]{3,2,1,0:T(8,128)S(1)}, f32[2,16,32,128]{3,2,1,0:T(8,128)}, u32[]{:S(2)}) %copy-start.1) | copy-done | bytes 524312
  2.7 0.0 copy-start.2
  2.7 1.0 %copy-done.2 = f32[2,16,32,128]{3,2,1,0:T(8,128)S(1)} copy-done((f32[2,16,32,128]{3,2,1,0:T(8,128)S(1)}, f32[2,16,32,128]{3,2,1,0:T(8,128)}, u32[]{:S(2)}) %copy-start.2) | copy-done | bytes 524312
  3.8 51.2 %shard_map.50 = (f32[2,16,32,128]{3,2,1,0:T(8,128)S(1)}, f32[2,16,32,128]{3,2,1,0:T(8,128)S(1)}) custom-call(f32[2,16,32,128]{3,2,1,0:T(8,128)S(1)} %copy-done, f32[2,16,32,128]{3,2,1,0:T(8,128)S(1)} %copy-done.1, f32[2,16,32,128]{3,2,1,0:T(8,128)S(1)} %copy-done.2), custom_call_target="tpu_custom_call" | custom-call | tf_op jit(solution)/shard_map/pallas_call | solution.py:390
  55.0 0.8 %copy.7 = f32[2,16,32,128]{3,2,1,0:T(8,128)} copy(f32[2,16,32,128]{3,2,1,0:T(8,128)S(1)} %get-tuple-element.4) | data formatting | bytes 1048576
  55.8 0.8 %copy.8 = f32[2,16,32,128]{3,2,1,0:T(8,128)} copy(f32[2,16,32,128]{3,2,1,0:T(8,128)S(1)} %get-tuple-element.5) | data formatting | bytes 1048576
Async XLA Ops:
  0.6 1.0 %copy-start = (f32[2,16,32,128]{3,2,1,0:T(8,128)S(1)}, f32[2,16,32,128]{3,2,1,0:T(8,128)}, u32[]{:S(2)}) copy-start(f32[2,16,32,128]{3,2,1,0:T(8,128)} %models.1) | copy-start | bytes 1572868
  1.7 1.0 %copy-start.1 = (f32[2,16,32,128]{3,2,1,0:T(8,128)S(1)}, f32[2,16,32,128]{3,2,1,0:T(8,128)}, u32[]{:S(2)}) copy-start(f32[2,16,32,128]{3,2,1,0:T(8,128)} %targets_in.1) | copy-start | bytes 1572868
  2.7 1.0 %copy-start.2 = (f32[2,16,32,128]{3,2,1,0:T(8,128)S(1)}, f32[2,16,32,128]{3,2,1,0:T(8,128)}, u32[]{:S(2)}) copy-start(f32[2,16,32,128]{3,2,1,0:T(8,128)} %weights_in.1) | copy-start | bytes 1572868
